TPU v7x, 128 devices: a whole 4x4x4 slice. The times are simulated.
128 devices in a mesh: row: 8 (over y, x_lo), col: 16 (over z, x_hi, core).
Axes of the slice: x: 4 (x_hi: 2, x_lo: 2; x = x_hi * 2 + x_lo), y: 4, z: 4, core: 2. Of those that a mesh axis runs over, the one named last changes fastest.
Arguments:
- gains: float32 [512, 8, 256], P(('row', 'col')), may hold values from -6 to 6
- coherency: bfloat16 [512, 512, 8, 1, 256], P('row', 'col'), may hold values from -6 to 6
- cotangent: bfloat16 [512, 512, 8, 1, 8], P('row', 'col'), may hold values from -0.099609375 to 0.099609375
- flags: int32 [512, 512, 1], P('row', 'col'), may hold values 0 or 1
- station_slot: int32 [512], replicated, may hold values from 0 to 511, as said below
Outputs:
- gain_grad: float32 [512, 8, 256], P(('row', 'col'))
Inputs may be any that keep to these rules, and one draw needn't show every extreme that they name: `station_slot`: each station appears in exactly one slot; in every aligned block of 4 consecutive slots the stations lie with 4 different holders, station s being held by the device of index s // 4 in the order of row+col.
All inputs are finite; a program needn't handle non-finite values. No bound on the sum of `flags` on one device may be relied on, other than what follows from the above.
Results may differ from a plain program's by a relative error of at most 0.0003.
Values sent between devices are 32-bit elements; how exact they have to be, the bound alone decides.
No kernel may reach another device: no remote copies, remote signals or barrier semaphores. Data moves between devices by JAX's collectives and lax.ppermute only.
A program may use at most 128 MiB of HBM per device.

v0:
```python
import jax
import jax.numpy as jnp
from jax import lax
from jax.sharding import PartitionSpec as P


def laid_out(blocks, dim):
    dims = list(blocks.shape[1:])
    dims[dim] *= blocks.shape[0]
    return jnp.moveaxis(blocks, 0, dim).reshape(dims)


def copy_for_each(x, axis):
    copies = jnp.broadcast_to(x, (lax.axis_size(axis), *x.shape))
    return lax.all_to_all(copies, axis, split_axis=0, concat_axis=0, tiled=True)


def gathered_copies(x, axis, dim):
    return laid_out(copy_for_each(x, axis), dim)


def split_up(x, dim, length):
    before, after = (x.shape[:dim], x.shape[dim + 1 :])
    return jnp.moveaxis(x.reshape(*before, length, -1, *after), dim, 0)


def summed_on_arrival(x, axis, dim):
    blocks = split_up(x, dim, lax.axis_size(axis))
    arrived = lax.all_to_all(blocks, axis, split_axis=0, concat_axis=0, tiled=True)
    return arrived.sum(axis=0)


def side_by_side(arrays, axis, split_dim, concat_dim, along):
    ends, at = ([], 0)
    for a in arrays[:-1]:
        at += a.shape[along]
        ends.append(at)
    both = jnp.concatenate(arrays, axis=along)
    return tuple(
        jnp.split(
            lax.all_to_all(both, axis, split_axis=split_dim, concat_axis=concat_dim, tiled=True),
            ends,
            axis=along,
        )
    )


def complex_product(first, second):
    return (
        first[0] * second[0] - first[1] * second[1],
        first[0] * second[1] + first[1] * second[0],
    )


def complex_sum(first, second):
    return (first[0] + second[0], first[1] + second[1])


def conjugate(element):
    return (element[0], -element[1])


def jones_product(first, second):
    return [
        complex_sum(
            complex_product(first[2 * row_index], second[column]),
            complex_product(first[2 * row_index + 1], second[2 + column]),
        )
        for row_index in (0, 1)
        for column in (0, 1)
    ]


def hermitian(matrix):
    return [conjugate(matrix[0]), conjugate(matrix[2]), conjugate(matrix[1]), conjugate(matrix[3])]


def as_complex(parts):
    return [(parts[0], parts[1]), (parts[2], parts[3]), (parts[4], parts[5]), (parts[6], parts[7])]


def as_parts(matrix):
    return [number for element in matrix for number in element]


def block_gradients(coherency, cotangent, flags, row_gains, col_gains):
    shape = coherency.shape
    directions = shape[4] // 8
    coherence = coherency.reshape(shape[:4] + (8, directions))
    weight = flags.astype(jnp.float32)[:, :, None, :, None]
    residual = as_complex(
        [
            cotangent[..., component].astype(jnp.float32)[..., None] * weight
            for component in range(8)
        ]
    )
    model_parts = as_complex(
        [coherence[..., component, :].astype(jnp.float32) for component in range(8)]
    )
    row_split = row_gains.reshape(row_gains.shape[0], row_gains.shape[1], 8, directions)
    col_split = col_gains.reshape(col_gains.shape[0], col_gains.shape[1], 8, directions)
    row_jones = as_complex([row_split[:, None, :, None, component, :] for component in range(8)])
    col_jones = as_complex([col_split[None, :, :, None, component, :] for component in range(8)])
    outgoing = jones_product(jones_product(residual, col_jones), hermitian(model_parts))
    row_side = jnp.stack([jnp.sum(part, axis=(1, 3)) for part in as_parts(outgoing)], axis=2)
    incoming = jones_product(jones_product(hermitian(residual), row_jones), model_parts)
    col_side = jnp.stack([jnp.sum(part, axis=(0, 3)) for part in as_parts(incoming)], axis=2)
    return (row_side.reshape(row_gains.shape), col_side.reshape(col_gains.shape))


def selector(identifiers, count):
    return (identifiers[:, None] == jnp.arange(count, dtype=jnp.int32)[None, :]).astype(jnp.float32)


def select_rows(table, values):
    return jnp.dot(
        table, values, precision=lax.Precision.HIGHEST, preferred_element_type=jnp.float32
    )


def shards(gains, coherency, cotangent, flags, station_slot):
    stations = station_slot.shape[0]
    share = gains.shape[0]
    flat = gains.shape[1] * gains.shape[2]
    row_total = lax.axis_size("row")
    col_total = lax.axis_size("col")
    groups = row_total * col_total
    row_place = lax.axis_index("row")
    col_place = lax.axis_index("col")
    device_place = row_place * col_total + col_place
    counting = jnp.arange(share, dtype=jnp.int32)
    slot_of = (
        jnp.zeros((stations,), jnp.int32)
        .at[station_slot]
        .set(jnp.arange(stations, dtype=jnp.int32))
    )
    own_blocks = jnp.take(slot_of, device_place * share + counting) // share
    col_target = own_blocks % row_total * col_total + own_blocks // row_total
    col_block = col_place * row_total + row_place
    row_holder = jnp.take(station_slot, device_place * share + counting) // share
    col_holder = jnp.take(station_slot, col_block * share + counting) // share
    row_count = coherency.shape[0]
    col_count = coherency.shape[1]
    row_ids = lax.dynamic_slice_in_dim(station_slot, row_place * row_count, row_count)
    col_ids = lax.dynamic_slice_in_dim(station_slot, col_place * col_count, col_count)
    col_piece = gathered_copies(gains, "col", 0)
    every_gain = lax.all_gather(col_piece, "row", axis=0, tiled=True)
    row_gains = jnp.take(every_gain, row_ids, axis=0)
    col_gains = jnp.take(every_gain, col_ids, axis=0)
    row_side, col_side = block_gradients(coherency, cotangent, flags, row_gains, col_gains)
    row_sum = summed_on_arrival(row_side, "col", 0)
    col_sum = summed_on_arrival(col_side, "row", 0)
    back_row = select_rows(selector(row_holder, groups).T, row_sum.reshape(share, flat))
    back_col = select_rows(selector(col_holder, groups).T, col_sum.reshape(share, flat))
    recv_row, recv_col = side_by_side((back_row, back_col), ("row", "col"), 0, 0, 1)
    result = select_rows(selector(own_blocks, groups), recv_row) + select_rows(
        selector(col_target, groups), recv_col
    )
    return result.reshape(gains.shape)


def solution(mesh):
    placed = (
        P(("row", "col"), None, None),
        P("row", "col", None, None, None),
        P("row", "col", None, None, None),
        P("row", "col", None),
        P(),
    )
    return jax.shard_map(
        shards, mesh=mesh, in_specs=placed, out_specs=P(("row", "col"), None, None), check_vma=False
    )
```

profile of v0, /device:TPU:1, one launch (start us, length us, event | category | flops | bytes accessed | tf_op | source)
XLA Modules:
  0.0 348.7 jit_solution(1977223666826343122)
XLA Ops:
  7.3 20.3 %all_to_all.27 = f32[16,4,8,256]{3,2,1,0:T(8,128)} all-to-all(f32[16,4,8,256]{3,2,1,0:T(8,128)S(1)} %broadcast_in_dim.52), channel_id=1, replica_groups=mesh['row'=8,'col'=16] {'col'}, dimensions={0} | all-to-all | bytes 1048576 | tf_op jit(solution)/shard_map/all_to_all | solution.py:15
  28.5 17.5 %copy.42 = bf16[64,32,8,1,256]{0,4,2,1,3:T(8,128)(2,1)} copy(bf16[64,32,8,1,256]{4,2,3,1,0:T(8,128)(2,1)} %param.8) | data formatting | bytes 16777216 | tf_op args[1]
  48.3 67.3 %all-gather.2.cloned.1.call-done = f32[512,8,256]{2,1,0:T(8,128)} async-done(((f32[64,8,256]{2,1,0:T(8,128)}), f32[512,8,256]{2,1,0:T(8,128)}) %all-gather.2.cloned.1.call-update) | async-done | bytes 4194320 | tf_op jit(solution)/shard_map/all_gather | solution.py:147
  115.5 2.8 gather_fusion.1
  118.9 8.5 %fusion.69 = f32[32,8,32]{2,1,0:T(8,128)S(1)} fusion(f32[64,8,32]{0,2,1:T(8,128)S(1)} %get-tuple-element.29, f32[64,8,32]{0,2,1:T(8,128)S(1)} %get-tuple-element.30, f32[64,8,32]{0,2,1:T(8,128)S(1)} %get-tuple-element.31, f32[64,8,32]{0,2,1:T(8,128)S(1)} %get-tuple-element.32, f32[64,8,32]{0,2,1:T(8,128)S(1)} %get-tuple-element.33, ...), kind=kLoop, calls=%fused_computation.127 | loop fusion | flops 20963328 | bytes 5013504 | tf_op jit(solution)/shard_map/reduce_sum | solution.py:107
  127.5 8.5 %fusion.66 = f32[32,8,32]{2,1,0:T(8,128)} fusion(f32[64,8,32]{0,2,1:T(8,128)S(1)} %get-tuple-element.29, f32[64,8,32]{0,2,1:T(8,128)S(1)} %get-tuple-element.30, f32[64,8,32]{0,2,1:T(8,128)S(1)} %get-tuple-element.31, f32[64,8,32]{0,2,1:T(8,128)S(1)} %get-tuple-element.32, f32[64,8,32]{0,2,1:T(8,128)S(1)} %get-tuple-element.33, ...), kind=kLoop, calls=%fused_computation.124 | loop fusion | flops 20963328 | bytes 5013504 | tf_op jit(solution)/shard_map/reduce_sum | solution.py:107
  136.0 6.9 %fusion.53 = f32[32,8,32]{2,1,0:T(8,128)} fusion(f32[64,8,32]{0,2,1:T(8,128)S(1)} %get-tuple-element.29, f32[64,8,32]{0,2,1:T(8,128)S(1)} %get-tuple-element.30, f32[64,8,32]{0,2,1:T(8,128)S(1)} %get-tuple-element.31, f32[64,8,32]{0,2,1:T(8,128)S(1)} %get-tuple-element.32, f32[64,8,32]{0,2,1:T(8,128)S(1)} %get-tuple-element.33, ...), kind=kLoop, calls=%fused_computation.111 | loop fusion | flops 20963328 | bytes 5013504 | tf_op jit(solution)/shard_map/reduce_sum | solution.py:107
  142.9 6.9 %fusion.50 = f32[32,8,32]{2,1,0:T(8,128)} fusion(f32[64,8,32]{0,2,1:T(8,128)S(1)} %get-tuple-element.29, f32[64,8,32]{0,2,1:T(8,128)S(1)} %get-tuple-element.30, f32[64,8,32]{0,2,1:T(8,128)S(1)} %get-tuple-element.31, f32[64,8,32]{0,2,1:T(8,128)S(1)} %get-tuple-element.32, f32[64,8,32]{0,2,1:T(8,128)S(1)} %get-tuple-element.33, ...), kind=kLoop, calls=%fused_computation.108 | loop fusion | flops 20963328 | bytes 5013504 | tf_op jit(solution)/shard_map/reduce_sum | solution.py:107
  149.8 3.4 gather_fusion
  155.3 11.8 %fusion.39 = f32[64,8,32]{0,2,1:T(8,128)S(1)} fusion(f32[64,32,8]{0,2,1:T(8,128)S(1)} %bitcast.387, f32[64,32,8]{0,2,1:T(8,128)S(1)} %bitcast.284, f32[64,32,8]{0,2,1:T(8,128)S(1)} %bitcast.383, f32[64,32,8]{0,2,1:T(8,128)S(1)} %bitcast.296, f32[32,8,32]{2,1,0:T(8,128)S(1)} %bitcast.308, f32[32,8,32]{2,1,0:T(8,128)S(1)} %bitcast.316, ...), kind=kLoop, calls=%fused_computation.97 | loop fusion | flops 22003712 | bytes 4784128 | tf_op jit(solution)/shard_map/reduce_sum | solution.py:105
  167.2 11.8 %fusion.36 = f32[64,8,32]{0,2,1:T(8,128)S(1)} fusion(f32[64,32,8]{0,2,1:T(8,128)S(1)} %bitcast.388, f32[64,32,8]{0,2,1:T(8,128)S(1)} %bitcast.285, f32[64,32,8]{0,2,1:T(8,128)S(1)} %bitcast.384, f32[64,32,8]{0,2,1:T(8,128)S(1)} %bitcast.297, f32[32,8,32]{2,1,0:T(8,128)S(1)} %bitcast.309, f32[32,8,32]{2,1,0:T(8,128)S(1)} %bitcast.317, ...), kind=kLoop, calls=%fused_computation.94 | loop fusion | flops 22003712 | bytes 4784128 | tf_op jit(solution)/shard_map/reduce_sum | solution.py:105
  179.0 11.8 %fusion.27 = f32[64,8,32]{0,2,1:T(8,128)S(1)} fusion(f32[64,32,8]{0,2,1:T(8,128)S(1)} %bitcast.389, f32[64,32,8]{0,2,1:T(8,128)S(1)} %bitcast.286, f32[64,32,8]{0,2,1:T(8,128)S(1)} %bitcast.385, f32[64,32,8]{0,2,1:T(8,128)S(1)} %bitcast.298, f32[32,8,32]{2,1,0:T(8,128)S(1)} %bitcast.310, f32[32,8,32]{2,1,0:T(8,128)S(1)} %bitcast.318, ...), kind=kLoop, calls=%fused_computation.85 | loop fusion | flops 22003712 | bytes 4784128 | tf_op jit(solution)/shard_map/reduce_sum | solution.py:105
  190.9 10.1 %fusion.24 = f32[64,8,32]{0,2,1:T(8,128)S(1)} fusion(f32[64,32,8]{0,2,1:T(8,128)S(1)} %bitcast.390, f32[64,32,8]{0,2,1:T(8,128)S(1)} %bitcast.287, f32[64,32,8]{0,2,1:T(8,128)S(1)} %bitcast.386, f32[64,32,8]{0,2,1:T(8,128)S(1)} %bitcast.299, f32[32,8,32]{2,1,0:T(8,128)S(1)} %bitcast.311, f32[32,8,32]{2,1,0:T(8,128)S(1)} %bitcast.319, ...), kind=kLoop, calls=%fused_computation.82 | loop fusion | flops 22003712 | bytes 4784128 | tf_op jit(solution)/shard_map/reduce_sum | solution.py:105
  201.0 10.7 %fusion.33 = f32[64,8,32]{0,2,1:T(8,128)} fusion(f32[32,8,32]{2,1,0:T(8,128)S(1)} %bitcast.312, f32[32,8,32]{2,1,0:T(8,128)S(1)} %bitcast.320, f32[32,8,32]{2,1,0:T(8,128)S(1)} %bitcast.328, f32[32,8,32]{2,1,0:T(8,128)S(1)} %bitcast.336, f32[32,8,32]{2,1,0:T(8,128)S(1)} %bitcast.344, f32[64,32,8]{0,2,1:T(8,128)S(1)} %bitcast.367, ...), kind=kLoop, calls=%fused_computation.91 | loop fusion | flops 22003712 | bytes 4784128 | tf_op jit(solution)/shard_map/reduce_sum | solution.py:105
  211.7 9.9 %fusion.18 = f32[64,8,32]{0,2,1:T(8,128)S(1)} fusion(f32[32,8,32]{2,1,0:T(8,128)S(1)} %bitcast.313, f32[32,8,32]{2,1,0:T(8,128)S(1)} %bitcast.321, f32[32,8,32]{2,1,0:T(8,128)S(1)} %bitcast.329, f32[32,8,32]{2,1,0:T(8,128)S(1)} %bitcast.337, f32[32,8,32]{2,1,0:T(8,128)S(1)} %bitcast.345, f32[64,32,8]{0,2,1:T(8,128)S(1)} %bitcast.368, ...), kind=kLoop, calls=%fused_computation.76 | loop fusion | flops 22003712 | bytes 4784128 | tf_op jit(solution)/shard_map/reduce_sum | solution.py:105
  221.6 6.2 %fusion.56 = f32[32,8,32]{2,1,0:T(8,128)S(1)} fusion(f32[64,32,8]{0,2,1:T(8,128)S(1)} %bitcast.379, f32[64,32,8]{0,2,1:T(8,128)S(1)} %bitcast.375, f32[64,8,32]{0,2,1:T(8,128)S(1)} %get-tuple-element.29, f32[64,8,32]{0,2,1:T(8,128)S(1)} %get-tuple-element.30, f32[64,8,32]{0,2,1:T(8,128)S(1)} %get-tuple-element.31, f32[64,8,32]{0,2,1:T(8,128)S(1)} %get-tuple-element.32, ...), kind=kLoop, calls=%fused_computation.114 | loop fusion | flops 20963328 | bytes 5013504 | tf_op jit(solution)/shard_map/reduce_sum | solution.py:107
  227.8 6.2 %fusion.72 = f32[32,8,32]{2,1,0:T(8,128)S(1)} fusion(f32[64,32,8]{0,2,1:T(8,128)S(1)} %bitcast.380, f32[64,32,8]{0,2,1:T(8,128)S(1)} %bitcast.376, f32[64,8,32]{0,2,1:T(8,128)S(1)} %get-tuple-element.29, f32[64,8,32]{0,2,1:T(8,128)S(1)} %get-tuple-element.30, f32[64,8,32]{0,2,1:T(8,128)S(1)} %get-tuple-element.31, f32[64,8,32]{0,2,1:T(8,128)S(1)} %get-tuple-element.32, ...), kind=kLoop, calls=%fused_computation.130 | loop fusion | flops 20963328 | bytes 5013504 | tf_op jit(solution)/shard_map/reduce_sum | solution.py:107
  234.0 6.2 %fusion.75 = f32[32,8,32]{2,1,0:T(8,128)S(1)} fusion(f32[64,32,8]{0,2,1:T(8,128)S(1)} %bitcast.381, f32[64,32,8]{0,2,1:T(8,128)S(1)} %bitcast.377, f32[64,8,32]{0,2,1:T(8,128)S(1)} %get-tuple-element.29, f32[64,8,32]{0,2,1:T(8,128)S(1)} %get-tuple-element.30, f32[64,8,32]{0,2,1:T(8,128)S(1)} %get-tuple-element.31, f32[64,8,32]{0,2,1:T(8,128)S(1)} %get-tuple-element.32, ...), kind=kLoop, calls=%fused_computation.133 | loop fusion | flops 20963328 | bytes 5013504 | tf_op jit(solution)/shard_map/reduce_sum | solution.py:107
  240.2 6.2 %fusion.59 = f32[32,8,32]{2,1,0:T(8,128)S(1)} fusion(f32[64,32,8]{0,2,1:T(8,128)S(1)} %bitcast.382, f32[64,32,8]{0,2,1:T(8,128)S(1)} %bitcast.378, f32[64,8,32]{0,2,1:T(8,128)S(1)} %get-tuple-element.29, f32[64,8,32]{0,2,1:T(8,128)S(1)} %get-tuple-element.30, f32[64,8,32]{0,2,1:T(8,128)S(1)} %get-tuple-element.31, f32[64,8,32]{0,2,1:T(8,128)S(1)} %get-tuple-element.32, ...), kind=kLoop, calls=%fused_computation.117 | loop fusion | flops 20963328 | bytes 5013504 | tf_op jit(solution)/shard_map/reduce_sum | solution.py:107
  246.5 9.9 %fusion.30 = f32[64,8,32]{0,2,1:T(8,128)S(1)} fusion(f32[32,8,32]{2,1,0:T(8,128)S(1)} %bitcast.314, f32[32,8,32]{2,1,0:T(8,128)S(1)} %bitcast.322, f32[32,8,32]{2,1,0:T(8,128)S(1)} %bitcast.330, f32[32,8,32]{2,1,0:T(8,128)S(1)} %bitcast.338, f32[32,8,32]{2,1,0:T(8,128)S(1)} %bitcast.346, f32[64,32,8]{0,2,1:T(8,128)S(1)} %bitcast.369, ...), kind=kLoop, calls=%fused_computation.88 | loop fusion | flops 22003712 | bytes 4784128 | tf_op jit(solution)/shard_map/reduce_sum | solution.py:105
  256.4 9.9 %fusion.21 = f32[64,8,32]{0,2,1:T(8,128)S(1)} fusion(f32[32,8,32]{2,1,0:T(8,128)S(1)} %bitcast.315, f32[32,8,32]{2,1,0:T(8,128)S(1)} %bitcast.323, f32[32,8,32]{2,1,0:T(8,128)S(1)} %bitcast.331, f32[32,8,32]{2,1,0:T(8,128)S(1)} %bitcast.339, f32[32,8,32]{2,1,0:T(8,128)S(1)} %bitcast.347, f32[64,32,8]{0,2,1:T(8,128)S(1)} %bitcast.370, ...), kind=kLoop, calls=%fused_computation.79 | loop fusion | flops 22003712 | bytes 4784128 | tf_op jit(solution)/shard_map/reduce_sum | solution.py:105
  266.4 1.6 stack.71
  269.0 3.8 %all-to-all-start.2 = ((f32[8,4,8,256]{3,2,1,0:T(8,128)}), f32[8,4,8,256]{3,2,1,0:T(8,128)S(1)}, u32[]{:S(2)}, u32[]{:S(2)}) async-start(f32[8,4,8,256]{3,2,1,0:T(8,128)} %reshape_reshape.7), calls=%async_computation.2 | async-start | bytes 524288 | tf_op jit(solution)/shard_map/all_to_all | solution.py:29
  273.0 1.8 copy.50
  276.2 2.8 all-to-all-done.2
  279.0 9.1 %all-to-all-start.1 = ((f32[16,4,8,256]{3,2,1,0:T(8,128)}), f32[16,4,8,256]{3,2,1,0:T(8,128)S(1)}, u32[]{:S(2)}, u32[]{:S(2)}) async-start(f32[16,4,8,256]{3,2,1,0:T(8,128)} %reshape_reshape.6), calls=%async_computation.1 | async-start | bytes 1048576 | tf_op jit(solution)/shard_map/all_to_all | solution.py:29
  289.5 9.7 %all-to-all-done.1 = f32[16,4,8,256]{3,2,1,0:T(8,128)S(1)} async-done(((f32[16,4,8,256]{3,2,1,0:T(8,128)}), f32[16,4,8,256]{3,2,1,0:T(8,128)S(1)}, u32[]{:S(2)}, u32[]{:S(2)}) %all-to-all-start.1) | async-done | bytes 524320 | tf_op jit(solution)/shard_map/all_to_all | solution.py:29
  300.2 3.5 %copy.52 = f32[128,1,4096]{2,1,0:T(1,128)} copy(f32[128,1,4096]{2,0,1:T(8,128)S(1)} %maximum_bitcast_fusion) | data formatting | bytes 4194304 | tf_op jit(solution)/shard_map/all_to_all | solution.py:41
  303.7 4.7 %all-to-all-start.3 = ((f32[128,1,4096]{2,1,0:T(1,128)}), f32[128,1,4096]{2,1,0:T(1,128)S(1)}, u32[]{:S(2)}, u32[]{:S(2)}) async-start(f32[128,1,4096]{2,1,0:T(1,128)} %copy.52), calls=%async_computation.3 | async-start | bytes 4194304 | tf_op jit(solution)/shard_map/all_to_all | solution.py:41
  308.5 2.4 scatter_custom_fusion
  311.6 27.1 %all-to-all-done.3 = f32[128,1,4096]{2,1,0:T(1,128)S(1)} async-done(((f32[128,1,4096]{2,1,0:T(1,128)}), f32[128,1,4096]{2,1,0:T(1,128)S(1)}, u32[]{:S(2)}, u32[]{:S(2)}) %all-to-all-start.3) | async-done | bytes 2097184 | tf_op jit(solution)/shard_map/all_to_all | solution.py:41
  338.7 1.6 copy.66
  (68 shorter events, 13.5 us)
Async XLA Ops:
  6.5 109.0 %all-gather.2.cloned.1.call-start = ((), (), s32[]{:S(2)}) async-start(), calls=%async_computation.4 | async-start | bytes 4718592 | tf_op jit(solution)/shard_map/all_gather | solution.py:147
  28.5 17.6 %copy-start.1 = (s32[512]{0:T(512)S(1)}, s32[512]{0:T(512)}, u32[]{:S(2)}) copy-start(s32[512]{0:T(512)} %param.11) | copy-start | bytes 6148
  28.5 18.4 %copy-start.2 = (bf16[64,32,8,1,8]{0,4,3,2,1:T(8,128)(2,1)S(1)}, bf16[64,32,8,1,8]{0,4,3,2,1:T(8,128)(2,1)}, u32[]{:S(2)}) copy-start(bf16[64,32,8,1,8]{0,4,3,2,1:T(8,128)(2,1)} %param.9) | copy-start | bytes 786436
  118.9 17.0 %copy-start = (bf16[64,32,8,1,256]{0,4,2,1,3:T(8,128)(2,1)S(1)}, bf16[64,32,8,1,256]{0,4,2,1,3:T(8,128)(2,1)}, u32[]{:S(2)}) copy-start(bf16[64,32,8,1,256]{0,4,2,1,3:T(8,128)(2,1)} %copy.42) | copy-start | bytes 25165828
  155.3 35.6 %slice-start = ((s8[16777216]{0:T(1024)(128)(4,1)}), s8[4194304]{0:T(1024)(128)(4,1)S(1)}, s32[]{:S(2)}) async-start(s8[16777216]{0:T(1024)(128)(4,1)} %bitcast.257), calls=%async_computation.5 | async-start | bytes 8388608
  155.3 35.6 %slice-start.1 = ((s8[16777216]{0:T(1024)(128)(4,1)}), s8[4194304]{0:T(1024)(128)(4,1)S(1)}, s32[]{:S(2)}) async-start(s8[16777216]{0:T(1024)(128)(4,1)} %bitcast.257), calls=%async_computation.6 | async-start | bytes 8388608
  167.2 23.7 %slice-start.2 = ((s8[16777216]{0:T(1024)(128)(4,1)}), s8[4194304]{0:T(1024)(128)(4,1)S(1)}, s32[]{:S(2)}) async-start(s8[16777216]{0:T(1024)(128)(4,1)} %bitcast.257), calls=%async_computation.7 | async-start | bytes 8388608
  179.0 11.9 %slice-start.3 = ((s8[16777216]{0:T(1024)(128)(4,1)}), s8[4194304]{0:T(1024)(128)(4,1)S(1)}, s32[]{:S(2)}) async-start(s8[16777216]{0:T(1024)(128)(4,1)} %bitcast.257), calls=%async_computation.8 | async-start | bytes 8388608
  256.4 10.0 %copy-start.3 = (f32[32,8,32]{2,1,0:T(8,128)S(1)}, f32[32,8,32]{2,1,0:T(8,128)}, u32[]{:S(2)}) copy-start(f32[32,8,32]{2,1,0:T(8,128)} %fusion.66) | copy-start | bytes 98308
  256.4 10.0 %copy-start.4 = (f32[32,8,32]{2,1,0:T(8,128)S(1)}, f32[32,8,32]{2,1,0:T(8,128)}, u32[]{:S(2)}) copy-start(f32[32,8,32]{2,1,0:T(8,128)} %fusion.53) | copy-start | bytes 98308
  256.4 10.0 %copy-start.5 = (f32[32,8,32]{2,1,0:T(8,128)S(1)}, f32[32,8,32]{2,1,0:T(8,128)}, u32[]{:S(2)}) copy-start(f32[32,8,32]{2,1,0:T(8,128)} %fusion.50) | copy-start | bytes 98308
  266.4 6.5 %copy-start.6 = (f32[64,8,32]{0,2,1:T(8,128)S(1)}, f32[64,8,32]{0,2,1:T(8,128)}, u32[]{:S(2)}) copy-start(f32[64,8,32]{0,2,1:T(8,128)} %fusion.33) | copy-start | bytes 196612
  269.0 10.0 %all-to-all-start.2 = ((f32[8,4,8,256]{3,2,1,0:T(8,128)}), f32[8,4,8,256]{3,2,1,0:T(8,128)S(1)}, u32[]{:S(2)}, u32[]{:S(2)}) async-start(f32[8,4,8,256]{3,2,1,0:T(8,128)} %reshape_reshape.7), calls=%async_computation.2 | async-start | bytes 524288 | tf_op jit(solution)/shard_map/all_to_all | solution.py:29
  279.0 20.2 %all-to-all-start.1 = ((f32[16,4,8,256]{3,2,1,0:T(8,128)}), f32[16,4,8,256]{3,2,1,0:T(8,128)S(1)}, u32[]{:S(2)}, u32[]{:S(2)}) async-start(f32[16,4,8,256]{3,2,1,0:T(8,128)} %reshape_reshape.6), calls=%async_computation.1 | async-start | bytes 1048576 | tf_op jit(solution)/shard_map/all_to_all | solution.py:29
  303.7 34.9 %all-to-all-start.3 = ((f32[128,1,4096]{2,1,0:T(1,128)}), f32[128,1,4096]{2,1,0:T(1,128)S(1)}, u32[]{:S(2)}, u32[]{:S(2)}) async-start(f32[128,1,4096]{2,1,0:T(1,128)} %copy.52), calls=%async_computation.3 | async-start | bytes 4194304 | tf_op jit(solution)/shard_map/all_to_all | solution.py:41
Sparse Core Ops, SparseCore 0:
  27.8 87.6 all-gather.1
where the time goes:
time: 350 us; the launch traced here: 349 us
  other arithmetic  145 us (41%)
  waiting for transfers between devices  107 us (31%)
  local copies, waits for them, and re-layouts  43.1 us (12%)
  blocking collectives  20.3 us (6%)
  starting transfers between devices  17.6 us (5%)
  between operations  13.9 us (4%)
    reduce_sum x8, other arithmetic, block_gradients(): jnp.sum(part, axis=(1, 3))  86.1 us
    all_gather x1, waiting for transfers between devices, shards(): every_gain = lax.all_gather(col_piece, 'row', axis=0, tiled=True)  67.3 us
    reduce_sum x8, other arithmetic, block_gradients(): jnp.sum(part, axis=(0, 3))  55.6 us
    all_to_all x1, waiting for transfers between devices, side_by_side(): lax.all_to_all(both, axis, split_axis=split_dim, concat_axis=concat_dim,...  27.1 us
    all_to_all x1, blocking collectives, copy_for_each(): return lax.all_to_all(copies, axis, split_axis=0, concat_axis=0, tiled=True)  20.3 us
    unnamed x34, local copies, waits for them, and re-layouts  19.9 us
    all_to_all x2, starting transfers between devices, summed_on_arrival(): lax.all_to_all(blocks, axis, split_axis=0, concat_axis=0, tiled=True)  12.9 us
    all_to_all x2, waiting for transfers between devices, summed_on_arrival(): lax.all_to_all(blocks, axis, split_axis=0, concat_axis=0, tiled=True)  12.5 us
  transfers between devices with their start and end apart: 4, of which 4 were waited for; matrix products, arithmetic and copies ran while one was open for 8% of the time, Pallas kernels for 0%

commit v1 on v0

--- a/solution.py
+++ b/solution.py
@@ -144,7 +144,10 @@
     row_ids = lax.dynamic_slice_in_dim(station_slot, row_place * row_count, row_count)
     col_ids = lax.dynamic_slice_in_dim(station_slot, col_place * col_count, col_count)
     col_piece = gathered_copies(gains, "col", 0)
-    every_gain = lax.all_gather(col_piece, "row", axis=0, tiled=True)
+    size = lax.axis_size("row")
+    pieces = jnp.stack([col_piece for _ in range(size)])
+    pieces = lax.all_to_all(pieces, "row", split_axis=0, concat_axis=0)
+    every_gain = jnp.concatenate(pieces, axis=0)
     row_gains = jnp.take(every_gain, row_ids, axis=0)
     col_gains = jnp.take(every_gain, col_ids, axis=0)
     row_side, col_side = block_gradients(coherency, cotangent, flags, row_gains, col_gains)

time: 350 us -> 305 us (0.87)
  waiting for transfers between devices: 107 us -> 65.2 us
  between operations: 13.9 us -> 0.46 us
  local copies, waits for them, and re-layouts: 43.1 us -> 48.1 us
    all_gather x1 -> x0, waiting for transfers between devices: 67.3 us -> none  [shards(): every_gain = lax.all_gather(col_piece, 'row', axis=0, tiled=True)]
    all_to_all x0 -> x1, waiting for transfers between devices: none -> 28.4 us  [shards(): pieces = lax.all_to_all(pieces, 'row', split_axis=0, concat_axis=0)]
    all_to_all x0 -> x1, starting transfers between devices: none -> 4.68 us  [shards(): pieces = lax.all_to_all(pieces, 'row', split_axis=0, concat_axis=0)]
    reduce_sum x8, other arithmetic: 86.1 us -> 89.8 us  [block_gradients(): jnp.sum(part, axis=(1, 3))]
    unnamed x34 -> x40, local copies, waits for them, and re-layouts: 19.9 us -> 22.6 us
  transfers between devices with their start and end apart: 4 -> 4, of which waited for: 4 -> 4; matrix products, arithmetic and copies ran while one was open for 8% -> 10% of each run, Pallas kernels for 0% -> 0%
where the time goes in v1:
time: 305 us; the launch traced here: 304 us
  other arithmetic  148 us (49%)
  waiting for transfers between devices  65.2 us (21%)
  local copies, waits for them, and re-layouts  48.1 us (16%)
  starting transfers between devices  20.3 us (7%)
  blocking collectives  20.2 us (7%)
    reduce_sum x8, other arithmetic, block_gradients(): jnp.sum(part, axis=(1, 3))  89.8 us
    reduce_sum x8, other arithmetic, block_gradients(): jnp.sum(part, axis=(0, 3))  55.6 us
    all_to_all x1, waiting for transfers between devices, shards(): pieces = lax.all_to_all(pieces, 'row', split_axis=0, concat_axis=0)  28.4 us
    all_to_all x1, waiting for transfers between devices, side_by_side(): lax.all_to_all(both, axis, split_axis=split_dim, concat_axis=concat_dim,...  27 us
    unnamed x40, local copies, waits for them, and re-layouts  22.6 us
    all_to_all x1, blocking collectives, copy_for_each(): return lax.all_to_all(copies, axis, split_axis=0, concat_axis=0, tiled=True)  20.2 us
    all_to_all x2, starting transfers between devices, summed_on_arrival(): lax.all_to_all(blocks, axis, split_axis=0, concat_axis=0, tiled=True)  10.2 us
    all_to_all x2, waiting for transfers between devices, summed_on_arrival(): lax.all_to_all(blocks, axis, split_axis=0, concat_axis=0, tiled=True)  9.88 us
  transfers between devices with their start and end apart: 4, of which 4 were waited for; matrix products, arithmetic and copies ran while one was open for 10% of the time, Pallas kernels for 0%

profile of v1, /device:TPU:1, one launch (start us, length us, event | category | flops | bytes accessed | tf_op | source)
XLA Modules:
  0.0 304.2 jit_solution(10075224547568082969)
XLA Ops:
  0.8 20.2 %all_to_all.32 = f32[16,4,8,256]{3,2,1,0:T(8,128)S(1)} all-to-all(f32[16,4,8,256]{3,2,1,0:T(8,128)S(1)} %broadcast_in_dim.52), channel_id=1, replica_groups=mesh['row'=8,'col'=16] {'col'}, dimensions={0} | all-to-all | bytes 1048576 | tf_op jit(solution)/shard_map/all_to_all | solution.py:15
  21.0 2.3 stack.57
  23.4 4.7 %all-to-all-start.1 = ((f32[8,64,8,256]{3,2,1,0:T(8,128)}), f32[8,64,8,256]{3,2,1,0:T(8,128)}, u32[]{:S(2)}, u32[]{:S(2)}) async-start(f32[8,64,8,256]{3,2,1,0:T(8,128)} %stack.57), calls=%async_computation.1 | async-start | bytes 8388608 | tf_op jit(solution)/shard_map/all_to_all | solution.py:149
  28.1 17.5 %copy.42 = bf16[64,32,8,1,256]{0,4,2,1,3:T(8,128)(2,1)} copy(bf16[64,32,8,1,256]{4,2,3,1,0:T(8,128)(2,1)} %param.8) | data formatting | bytes 16777216 | tf_op args[1]
  47.9 28.4 %all-to-all-done.1 = f32[8,64,8,256]{3,2,1,0:T(8,128)} async-done(((f32[8,64,8,256]{3,2,1,0:T(8,128)}), f32[8,64,8,256]{3,2,1,0:T(8,128)}, u32[]{:S(2)}, u32[]{:S(2)}) %all-to-all-start.1) | async-done | bytes 4194336 | tf_op jit(solution)/shard_map/all_to_all | solution.py:149
  76.3 2.8 gather_fusion.1
  79.7 8.5 %fusion.69 = f32[32,8,32]{2,1,0:T(8,128)S(1)} fusion(f32[64,8,32]{0,2,1:T(8,128)S(1)} %get-tuple-element.29, f32[64,8,32]{0,2,1:T(8,128)S(1)} %get-tuple-element.30, f32[64,8,32]{0,2,1:T(8,128)S(1)} %get-tuple-element.31, f32[64,8,32]{0,2,1:T(8,128)S(1)} %get-tuple-element.32, f32[64,8,32]{0,2,1:T(8,128)S(1)} %get-tuple-element.33, ...), kind=kLoop, calls=%fused_computation.127 | loop fusion | flops 20963328 | bytes 5013504 | tf_op jit(solution)/shard_map/reduce_sum | solution.py:107
  88.2 8.5 %fusion.66 = f32[32,8,32]{2,1,0:T(8,128)} fusion(f32[64,8,32]{0,2,1:T(8,128)S(1)} %get-tuple-element.29, f32[64,8,32]{0,2,1:T(8,128)S(1)} %get-tuple-element.30, f32[64,8,32]{0,2,1:T(8,128)S(1)} %get-tuple-element.31, f32[64,8,32]{0,2,1:T(8,128)S(1)} %get-tuple-element.32, f32[64,8,32]{0,2,1:T(8,128)S(1)} %get-tuple-element.33, ...), kind=kLoop, calls=%fused_computation.124 | loop fusion | flops 20963328 | bytes 5013504 | tf_op jit(solution)/shard_map/reduce_sum | solution.py:107
  96.7 6.9 %fusion.53 = f32[32,8,32]{2,1,0:T(8,128)} fusion(f32[64,8,32]{0,2,1:T(8,128)S(1)} %get-tuple-element.29, f32[64,8,32]{0,2,1:T(8,128)S(1)} %get-tuple-element.30, f32[64,8,32]{0,2,1:T(8,128)S(1)} %get-tuple-element.31, f32[64,8,32]{0,2,1:T(8,128)S(1)} %get-tuple-element.32, f32[64,8,32]{0,2,1:T(8,128)S(1)} %get-tuple-element.33, ...), kind=kLoop, calls=%fused_computation.111 | loop fusion | flops 20963328 | bytes 5013504 | tf_op jit(solution)/shard_map/reduce_sum | solution.py:107
  103.7 6.9 %fusion.50 = f32[32,8,32]{2,1,0:T(8,128)} fusion(f32[64,8,32]{0,2,1:T(8,128)S(1)} %get-tuple-element.29, f32[64,8,32]{0,2,1:T(8,128)S(1)} %get-tuple-element.30, f32[64,8,32]{0,2,1:T(8,128)S(1)} %get-tuple-element.31, f32[64,8,32]{0,2,1:T(8,128)S(1)} %get-tuple-element.32, f32[64,8,32]{0,2,1:T(8,128)S(1)} %get-tuple-element.33, ...), kind=kLoop, calls=%fused_computation.108 | loop fusion | flops 20963328 | bytes 5013504 | tf_op jit(solution)/shard_map/reduce_sum | solution.py:107
  110.6 3.4 %gather_fusion = f32[32,8,256]{2,1,0:T(8,128)} fusion(f32[512,8,256]{2,1,0:T(8,128)} %bitcast.3, s32[1024]{0:T(1024)S(1)} %get-tuple-element.49), kind=kCustom, calls=%fused_computation.3 | custom fusion | bytes 524416 | tf_op jit(solution)/shard_map/jit(_take)/gather | solution.py:152
  116.1 11.8 %fusion.39 = f32[64,8,32]{0,2,1:T(8,128)S(1)} fusion(f32[64,32,8]{0,2,1:T(8,128)S(1)} %bitcast.388, f32[64,32,8]{0,2,1:T(8,128)S(1)} %bitcast.285, f32[64,32,8]{0,2,1:T(8,128)S(1)} %bitcast.384, f32[64,32,8]{0,2,1:T(8,128)S(1)} %bitcast.297, f32[32,8,32]{2,1,0:T(8,128)S(1)} %bitcast.309, f32[32,8,32]{2,1,0:T(8,128)S(1)} %bitcast.317, ...), kind=kLoop, calls=%fused_computation.97 | loop fusion | flops 22003712 | bytes 4784128 | tf_op jit(solution)/shard_map/reduce_sum | solution.py:105
  128.0 12.4 %fusion.36 = f32[64,8,32]{0,2,1:T(8,128)} fusion(f32[64,32,8]{0,2,1:T(8,128)S(1)} %bitcast.389, f32[64,32,8]{0,2,1:T(8,128)S(1)} %bitcast.286, f32[64,32,8]{0,2,1:T(8,128)S(1)} %bitcast.385, f32[64,32,8]{0,2,1:T(8,128)S(1)} %bitcast.298, f32[32,8,32]{2,1,0:T(8,128)S(1)} %bitcast.310, f32[32,8,32]{2,1,0:T(8,128)S(1)} %bitcast.318, ...), kind=kLoop, calls=%fused_computation.94 | loop fusion | flops 22003712 | bytes 4784128 | tf_op jit(solution)/shard_map/reduce_sum | solution.py:105
  140.4 11.8 %fusion.27 = f32[64,8,32]{0,2,1:T(8,128)S(1)} fusion(f32[64,32,8]{0,2,1:T(8,128)S(1)} %bitcast.390, f32[64,32,8]{0,2,1:T(8,128)S(1)} %bitcast.287, f32[64,32,8]{0,2,1:T(8,128)S(1)} %bitcast.386, f32[64,32,8]{0,2,1:T(8,128)S(1)} %bitcast.299, f32[32,8,32]{2,1,0:T(8,128)S(1)} %bitcast.311, f32[32,8,32]{2,1,0:T(8,128)S(1)} %bitcast.319, ...), kind=kLoop, calls=%fused_computation.85 | loop fusion | flops 22003712 | bytes 4784128 | tf_op jit(solution)/shard_map/reduce_sum | solution.py:105
  152.3 10.9 %fusion.24 = f32[64,8,32]{0,2,1:T(8,128)} fusion(f32[64,32,8]{0,2,1:T(8,128)S(1)} %bitcast.391, f32[64,32,8]{0,2,1:T(8,128)S(1)} %bitcast.288, f32[64,32,8]{0,2,1:T(8,128)S(1)} %bitcast.387, f32[64,32,8]{0,2,1:T(8,128)S(1)} %bitcast.300, f32[32,8,32]{2,1,0:T(8,128)S(1)} %bitcast.312, f32[32,8,32]{2,1,0:T(8,128)S(1)} %bitcast.320, ...), kind=kLoop, calls=%fused_computation.82 | loop fusion | flops 22003712 | bytes 4784128 | tf_op jit(solution)/shard_map/reduce_sum | solution.py:105
  163.1 10.7 %fusion.33 = f32[64,8,32]{0,2,1:T(8,128)} fusion(f32[32,8,32]{2,1,0:T(8,128)S(1)} %bitcast.313, f32[32,8,32]{2,1,0:T(8,128)S(1)} %bitcast.321, f32[32,8,32]{2,1,0:T(8,128)S(1)} %bitcast.329, f32[32,8,32]{2,1,0:T(8,128)S(1)} %bitcast.337, f32[32,8,32]{2,1,0:T(8,128)S(1)} %bitcast.345, f32[64,32,8]{0,2,1:T(8,128)S(1)} %bitcast.368, ...), kind=kLoop, calls=%fused_computation.91 | loop fusion | flops 22003712 | bytes 4784128 | tf_op jit(solution)/shard_map/reduce_sum | solution.py:105
  173.8 10.7 %fusion.18 = f32[64,8,32]{0,2,1:T(8,128)} fusion(f32[32,8,32]{2,1,0:T(8,128)S(1)} %bitcast.314, f32[32,8,32]{2,1,0:T(8,128)S(1)} %bitcast.322, f32[32,8,32]{2,1,0:T(8,128)S(1)} %bitcast.330, f32[32,8,32]{2,1,0:T(8,128)S(1)} %bitcast.338, f32[32,8,32]{2,1,0:T(8,128)S(1)} %bitcast.346, f32[64,32,8]{0,2,1:T(8,128)S(1)} %bitcast.369, ...), kind=kLoop, calls=%fused_computation.76 | loop fusion | flops 22003712 | bytes 4784128 | tf_op jit(solution)/shard_map/reduce_sum | solution.py:105
  184.5 6.2 %fusion.56 = f32[32,8,32]{2,1,0:T(8,128)S(1)} fusion(f32[64,32,8]{0,2,1:T(8,128)S(1)} %bitcast.380, f32[64,32,8]{0,2,1:T(8,128)S(1)} %bitcast.376, f32[64,8,32]{0,2,1:T(8,128)S(1)} %get-tuple-element.29, f32[64,8,32]{0,2,1:T(8,128)S(1)} %get-tuple-element.30, f32[64,8,32]{0,2,1:T(8,128)S(1)} %get-tuple-element.31, f32[64,8,32]{0,2,1:T(8,128)S(1)} %get-tuple-element.32, ...), kind=kLoop, calls=%fused_computation.114 | loop fusion | flops 20963328 | bytes 5013504 | tf_op jit(solution)/shard_map/reduce_sum | solution.py:107
  190.7 6.2 %fusion.72 = f32[32,8,32]{2,1,0:T(8,128)S(1)} fusion(f32[64,32,8]{0,2,1:T(8,128)S(1)} %bitcast.381, f32[64,32,8]{0,2,1:T(8,128)S(1)} %bitcast.377, f32[64,8,32]{0,2,1:T(8,128)S(1)} %get-tuple-element.29, f32[64,8,32]{0,2,1:T(8,128)S(1)} %get-tuple-element.30, f32[64,8,32]{0,2,1:T(8,128)S(1)} %get-tuple-element.31, f32[64,8,32]{0,2,1:T(8,128)S(1)} %get-tuple-element.32, ...), kind=kLoop, calls=%fused_computation.130 | loop fusion | flops 20963328 | bytes 5013504 | tf_op jit(solution)/shard_map/reduce_sum | solution.py:107
  196.9 6.2 %fusion.75 = f32[32,8,32]{2,1,0:T(8,128)S(1)} fusion(f32[64,32,8]{0,2,1:T(8,128)S(1)} %bitcast.382, f32[64,32,8]{0,2,1:T(8,128)S(1)} %bitcast.378, f32[64,8,32]{0,2,1:T(8,128)S(1)} %get-tuple-element.29, f32[64,8,32]{0,2,1:T(8,128)S(1)} %get-tuple-element.30, f32[64,8,32]{0,2,1:T(8,128)S(1)} %get-tuple-element.31, f32[64,8,32]{0,2,1:T(8,128)S(1)} %get-tuple-element.32, ...), kind=kLoop, calls=%fused_computation.133 | loop fusion | flops 20963328 | bytes 5013504 | tf_op jit(solution)/shard_map/reduce_sum | solution.py:107
  203.1 6.2 %fusion.59 = f32[32,8,32]{2,1,0:T(8,128)S(1)} fusion(f32[64,32,8]{0,2,1:T(8,128)S(1)} %bitcast.383, f32[64,32,8]{0,2,1:T(8,128)S(1)} %bitcast.379, f32[64,8,32]{0,2,1:T(8,128)S(1)} %get-tuple-element.29, f32[64,8,32]{0,2,1:T(8,128)S(1)} %get-tuple-element.30, f32[64,8,32]{0,2,1:T(8,128)S(1)} %get-tuple-element.31, f32[64,8,32]{0,2,1:T(8,128)S(1)} %get-tuple-element.32, ...), kind=kLoop, calls=%fused_computation.117 | loop fusion | flops 20963328 | bytes 5013504 | tf_op jit(solution)/shard_map/reduce_sum | solution.py:107
  209.3 10.7 %fusion.30 = f32[64,8,32]{0,2,1:T(8,128)} fusion(f32[32,8,32]{2,1,0:T(8,128)S(1)} %bitcast.315, f32[32,8,32]{2,1,0:T(8,128)S(1)} %bitcast.323, f32[32,8,32]{2,1,0:T(8,128)S(1)} %bitcast.331, f32[32,8,32]{2,1,0:T(8,128)S(1)} %bitcast.339, f32[32,8,32]{2,1,0:T(8,128)S(1)} %bitcast.347, f32[64,32,8]{0,2,1:T(8,128)S(1)} %bitcast.370, ...), kind=kLoop, calls=%fused_computation.88 | loop fusion | flops 22003712 | bytes 4784128 | tf_op jit(solution)/shard_map/reduce_sum | solution.py:105
  220.1 10.7 %fusion.21 = f32[64,8,32]{0,2,1:T(8,128)} fusion(f32[32,8,32]{2,1,0:T(8,128)S(1)} %bitcast.316, f32[32,8,32]{2,1,0:T(8,128)S(1)} %bitcast.324, f32[32,8,32]{2,1,0:T(8,128)S(1)} %bitcast.332, f32[32,8,32]{2,1,0:T(8,128)S(1)} %bitcast.340, f32[32,8,32]{2,1,0:T(8,128)S(1)} %bitcast.348, f32[64,32,8]{0,2,1:T(8,128)S(1)} %bitcast.371, ...), kind=kLoop, calls=%fused_computation.79 | loop fusion | flops 22003712 | bytes 4784128 | tf_op jit(solution)/shard_map/reduce_sum | solution.py:105
  233.4 4.0 %all-to-all-start.3 = ((f32[8,4,8,256]{3,2,1,0:T(8,128)}), f32[8,4,8,256]{3,2,1,0:T(8,128)S(1)}, u32[]{:S(2)}, u32[]{:S(2)}) async-start(f32[8,4,8,256]{3,2,1,0:T(8,128)} %reshape_reshape.7), calls=%async_computation.3 | async-start | bytes 524288 | tf_op jit(solution)/shard_map/all_to_all | solution.py:29
  240.4 1.8 copy.50
  243.7 6.2 %all-to-all-start.2 = ((f32[16,4,8,256]{3,2,1,0:T(8,128)}), f32[16,4,8,256]{3,2,1,0:T(8,128)S(1)}, u32[]{:S(2)}, u32[]{:S(2)}) async-start(f32[16,4,8,256]{3,2,1,0:T(8,128)} %reshape_reshape.6), calls=%async_computation.2 | async-start | bytes 1048576 | tf_op jit(solution)/shard_map/all_to_all | solution.py:29
  251.4 9.7 %all-to-all-done.2 = f32[16,4,8,256]{3,2,1,0:T(8,128)S(1)} async-done(((f32[16,4,8,256]{3,2,1,0:T(8,128)}), f32[16,4,8,256]{3,2,1,0:T(8,128)S(1)}, u32[]{:S(2)}, u32[]{:S(2)}) %all-to-all-start.2) | async-done | bytes 524320 | tf_op jit(solution)/shard_map/all_to_all | solution.py:29
  262.1 3.5 %copy.52 = f32[128,1,4096]{2,1,0:T(1,128)} copy(f32[128,1,4096]{2,0,1:T(8,128)S(1)} %maximum_bitcast_fusion) | data formatting | bytes 4194304 | tf_op jit(solution)/shard_map/all_to_all | solution.py:41
  265.6 5.4 %all-to-all-start.4 = ((f32[128,1,4096]{2,1,0:T(1,128)}), f32[128,1,4096]{2,1,0:T(1,128)S(1)}, u32[]{:S(2)}, u32[]{:S(2)}) async-start(f32[128,1,4096]{2,1,0:T(1,128)} %copy.52), calls=%async_computation.4 | async-start | bytes 4194304 | tf_op jit(solution)/shard_map/all_to_all | solution.py:41
  271.0 2.4 scatter_custom_fusion
  274.1 27.0 %all-to-all-done.4 = f32[128,1,4096]{2,1,0:T(1,128)S(1)} async-done(((f32[128,1,4096]{2,1,0:T(1,128)}), f32[128,1,4096]{2,1,0:T(1,128)S(1)}, u32[]{:S(2)}, u32[]{:S(2)}) %all-to-all-start.4) | async-done | bytes 2097184 | tf_op jit(solution)/shard_map/all_to_all | solution.py:41
  301.1 1.6 copy.66
  (74 shorter events, 17.2 us)
Async XLA Ops:
  23.4 4.7 %copy-start.9 = (s32[64,32,1]{0,2,1:T(1,128)S(1)}, s32[64,32,1]{0,2,1:T(1,128)}, u32[]{:S(2)}) copy-start(s32[64,32,1]{0,2,1:T(1,128)} %param.10) | copy-start | bytes 24580
  23.4 52.9 %all-to-all-start.1 = ((f32[8,64,8,256]{3,2,1,0:T(8,128)}), f32[8,64,8,256]{3,2,1,0:T(8,128)}, u32[]{:S(2)}, u32[]{:S(2)}) async-start(f32[8,64,8,256]{3,2,1,0:T(8,128)} %stack.57), calls=%async_computation.1 | async-start | bytes 8388608 | tf_op jit(solution)/shard_map/all_to_all | solution.py:149
  28.1 17.5 %copy-start.1 = (s32[512]{0:T(512)S(1)}, s32[512]{0:T(512)}, u32[]{:S(2)}) copy-start(s32[512]{0:T(512)} %param.11) | copy-start | bytes 6148
  28.1 18.4 %copy-start.2 = (bf16[64,32,8,1,8]{0,4,3,2,1:T(8,128)(2,1)S(1)}, bf16[64,32,8,1,8]{0,4,3,2,1:T(8,128)(2,1)}, u32[]{:S(2)}) copy-start(bf16[64,32,8,1,8]{0,4,3,2,1:T(8,128)(2,1)} %param.9) | copy-start | bytes 786436
  79.7 17.0 %copy-start = (bf16[64,32,8,1,256]{0,4,2,1,3:T(8,128)(2,1)S(1)}, bf16[64,32,8,1,256]{0,4,2,1,3:T(8,128)(2,1)}, u32[]{:S(2)}) copy-start(bf16[64,32,8,1,256]{0,4,2,1,3:T(8,128)(2,1)} %copy.42) | copy-start | bytes 25165828
  116.1 36.1 %slice-start = ((s8[16777216]{0:T(1024)(128)(4,1)}), s8[4194304]{0:T(1024)(128)(4,1)S(1)}, s32[]{:S(2)}) async-start(s8[16777216]{0:T(1024)(128)(4,1)} %bitcast.258), calls=%async_computation.5 | async-start | bytes 8388608
  116.1 36.1 %slice-start.1 = ((s8[16777216]{0:T(1024)(128)(4,1)}), s8[4194304]{0:T(1024)(128)(4,1)S(1)}, s32[]{:S(2)}) async-start(s8[16777216]{0:T(1024)(128)(4,1)} %bitcast.258), calls=%async_computation.6 | async-start | bytes 8388608
  127.9 24.3 %slice-start.2 = ((s8[16777216]{0:T(1024)(128)(4,1)}), s8[4194304]{0:T(1024)(128)(4,1)S(1)}, s32[]{:S(2)}) async-start(s8[16777216]{0:T(1024)(128)(4,1)} %bitcast.258), calls=%async_computation.7 | async-start | bytes 8388608
  140.4 11.9 %slice-start.3 = ((s8[16777216]{0:T(1024)(128)(4,1)}), s8[4194304]{0:T(1024)(128)(4,1)S(1)}, s32[]{:S(2)}) async-start(s8[16777216]{0:T(1024)(128)(4,1)} %bitcast.258), calls=%async_computation.8 | async-start | bytes 8388608
  220.1 10.7 %copy-start.3 = (f32[32,8,32]{2,1,0:T(8,128)S(1)}, f32[32,8,32]{2,1,0:T(8,128)}, u32[]{:S(2)}) copy-start(f32[32,8,32]{2,1,0:T(8,128)} %fusion.66) | copy-start | bytes 98308
  220.1 10.7 %copy-start.4 = (f32[32,8,32]{2,1,0:T(8,128)S(1)}, f32[32,8,32]{2,1,0:T(8,128)}, u32[]{:S(2)}) copy-start(f32[32,8,32]{2,1,0:T(8,128)} %fusion.53) | copy-start | bytes 98308
  220.1 10.7 %copy-start.5 = (f32[32,8,32]{2,1,0:T(8,128)S(1)}, f32[32,8,32]{2,1,0:T(8,128)}, u32[]{:S(2)}) copy-start(f32[32,8,32]{2,1,0:T(8,128)} %fusion.50) | copy-start | bytes 98308
  230.8 8.6 %copy-start.8 = (f32[64,8,32]{0,2,1:T(8,128)S(1)}, f32[64,8,32]{0,2,1:T(8,128)}, u32[]{:S(2)}) copy-start(f32[64,8,32]{0,2,1:T(8,128)} %fusion.18) | copy-start | bytes 196612
  230.8 9.5 %copy-start.7 = (f32[64,8,32]{0,2,1:T(8,128)S(1)}, f32[64,8,32]{0,2,1:T(8,128)}, u32[]{:S(2)}) copy-start(f32[64,8,32]{0,2,1:T(8,128)} %fusion.36) | copy-start | bytes 196612
  230.8 9.6 %copy-start.6 = (f32[64,8,32]{0,2,1:T(8,128)S(1)}, f32[64,8,32]{0,2,1:T(8,128)}, u32[]{:S(2)}) copy-start(f32[64,8,32]{0,2,1:T(8,128)} %fusion.24) | copy-start | bytes 196612
  233.4 10.3 %all-to-all-start.3 = ((f32[8,4,8,256]{3,2,1,0:T(8,128)}), f32[8,4,8,256]{3,2,1,0:T(8,128)S(1)}, u32[]{:S(2)}, u32[]{:S(2)}) async-start(f32[8,4,8,256]{3,2,1,0:T(8,128)} %reshape_reshape.7), calls=%async_computation.3 | async-start | bytes 524288 | tf_op jit(solution)/shard_map/all_to_all | solution.py:29
  243.7 17.4 %all-to-all-start.2 = ((f32[16,4,8,256]{3,2,1,0:T(8,128)}), f32[16,4,8,256]{3,2,1,0:T(8,128)S(1)}, u32[]{:S(2)}, u32[]{:S(2)}) async-start(f32[16,4,8,256]{3,2,1,0:T(8,128)} %reshape_reshape.6), calls=%async_computation.2 | async-start | bytes 1048576 | tf_op jit(solution)/shard_map/all_to_all | solution.py:29
  265.6 35.5 %all-to-all-start.4 = ((f32[128,1,4096]{2,1,0:T(1,128)}), f32[128,1,4096]{2,1,0:T(1,128)S(1)}, u32[]{:S(2)}, u32[]{:S(2)}) async-start(f32[128,1,4096]{2,1,0:T(1,128)} %copy.52), calls=%async_computation.4 | async-start | bytes 4194304 | tf_op jit(solution)/shard_map/all_to_all | solution.py:41
